TPU v7x, 32 devices: a whole 2x2x4 slice. The times are simulated.
32 devices in a mesh: chain: 4 (over x, core), blk: 8 (over z, y).
Axes of the slice: x: 2, y: 2, z: 4, core: 2. Of those that a mesh axis runs over, the one named last changes fastest.
Arguments:
- schur: bfloat16 [8192, 2048], P(('chain', 'blk')), as said below
- coupling: bfloat16 [8192, 2048], P(('chain', 'blk')), may hold values from -0.0625 to 0.0625
- next_diag: float32 [8192, 2048], P(('chain', 'blk')), as said below
Outputs:
- factor: float32 [8192, 2048], P(('chain', 'blk'))
- next_schur: float32 [8192, 2048], P(('chain', 'blk'))
Inputs may be any that keep to these rules, and one draw needn't show every extreme that they name: `schur`: every slab's block is symmetric positive definite. `next_diag`: every slab's block is symmetric positive definite.
All inputs are finite; a program needn't handle non-finite values.
Results may differ from a plain program's by a relative error of at most 0.0034.
Values may be sent and summed in bfloat16 or wider, within the bound.
A program may use at most 128 MiB of HBM per device.

v0:
```python
import jax
import jax.numpy as jnp
from jax import lax
from jax.sharding import PartitionSpec as P


def passed_along(value, axis, steps):
    count = lax.axis_size(axis)
    initial, last = (max(0, -steps), min(count, count - steps))
    return lax.ppermute(value, axis, [(source, source + steps) for source in range(initial, last)])


def panel_width(total):
    return min(512, total)


def blocked_cholesky(matrix):
    total = matrix.shape[0]
    width = panel_width(total)
    trailing = matrix
    columns = []
    for start in range(0, total, width):
        head = trailing[:width, :width]
        head_lower = jnp.linalg.cholesky(head)
        if start + width < total:
            below = trailing[width:, :width]
            below_lower = lax.linalg.triangular_solve(
                head_lower, below, left_side=False, lower=True, transpose_a=True
            )
            trailing = trailing[width:, width:] - jnp.dot(
                below_lower, below_lower.T, precision=lax.Precision.HIGHEST
            )
            panel = jnp.concatenate([head_lower, below_lower], axis=0)
        else:
            panel = head_lower
        columns.append(jnp.concatenate([jnp.zeros((start, width), jnp.float32), panel], axis=0))
    return jnp.concatenate(columns, axis=1)


def blocked_forward(lower, right_side):
    total = lower.shape[0]
    width = panel_width(total)
    remaining = right_side
    pieces = []
    for start in range(0, total, width):
        head_lower = lower[start : start + width, start : start + width]
        piece = lax.linalg.triangular_solve(
            head_lower, remaining[:width], left_side=True, lower=True
        )
        pieces.append(piece)
        if start + width < total:
            remaining = remaining[width:] - jnp.dot(
                lower[start + width :, start : start + width],
                piece,
                precision=lax.Precision.HIGHEST,
            )
    return jnp.concatenate(pieces, axis=0)


def update_rows_from(solved_local, column_piece):
    return lax.dot_general(
        solved_local, column_piece, (((0,), (0,)), ((), ())), preferred_element_type=jnp.float32
    )


def local(schur, coupling, next_diag):
    row_count = schur.shape[0]
    whole_schur = lax.all_gather(schur, "blk", axis=0, tiled=True).astype(jnp.float32)
    lower = blocked_cholesky(whole_schur)
    row_start = lax.axis_index("blk") * row_count
    my_rows = lax.dynamic_slice_in_dim(lower, row_start, row_count, 0)
    solved = blocked_forward(lower, coupling.astype(jnp.float32).T).astype(jnp.bfloat16)
    arrived = passed_along(solved, "chain", 1)
    incoming = update_rows_from(arrived, lax.all_gather(arrived, "blk", axis=1, tiled=True))
    return (my_rows, next_diag - incoming)


def solution(mesh):
    placed = (P(("chain", "blk"), None), P(("chain", "blk"), None), P(("chain", "blk"), None))
    return jax.shard_map(
        local,
        mesh=mesh,
        in_specs=placed,
        out_specs=(P(("chain", "blk"), None), P(("chain", "blk"), None)),
        check_vma=False,
    )
```

profile of v0, /device:TPU:0, one launch (start us, length us, event | category | flops | bytes accessed | tf_op | source)
XLA Modules:
  0.0 1040.7 jit_solution(9801016762331098428)
XLA Ops:
  11.7 126.6 %all-gather.3.cloned.1.call-done = bf16[2048,2048]{0,1:T(8,128)(2,1)} async-done(((bf16[256,2048]{0,1:T(8,128)(2,1)}), bf16[2048,2048]{0,1:T(8,128)(2,1)}) %all-gather.3.cloned.1.call-update) | async-done | bytes 8388624 | tf_op jit(solution)/shard_map/all_gather | solution.py:68
  139.8 11.2 %convert_element_type.2 = f32[2048,2048]{0,1:T(8,128)} convert(bf16[2048,2048]{0,1:T(8,128)(2,1)} %all-gather.3.cloned.1.call-done) | non-fusion elementwise | flops 4194304 | bytes 25165824 | tf_op jit(solution)/shard_map/convert_element_type | solution.py:68
  152.5 11.7 %cholesky.462 = f32[128,128]{1,0:T(8,128)S(1)} custom-call(f32[128,128]{1,0:T(8,128)S(1)} %cholesky.746), custom_call_target="Cholesky" | custom-call | tf_op jit(solution)/shard_map/jit(cholesky)/cholesky | solution.py:24
  164.2 9.8 custom-call.47
  174.9 11.9 %cholesky.481 = f32[128,128]{1,0:T(8,128)S(1)} custom-call(f32[128,128]{1,0:T(8,128)S(1)} %cholesky.750), custom_call_target="Cholesky" | custom-call | tf_op jit(solution)/shard_map/jit(cholesky)/cholesky | solution.py:24
  186.8 9.8 custom-call.48
  197.3 11.7 %cholesky.502 = f32[128,128]{1,0:T(8,128)S(1)} custom-call(f32[128,128]{1,0:T(8,128)S(1)} %cholesky.755), custom_call_target="Cholesky" | custom-call | tf_op jit(solution)/shard_map/jit(cholesky)/cholesky | solution.py:24
  209.7 9.8 custom-call.49
  220.1 23.1 %cholesky.519 = f32[128,128]{1,0:T(8,128)S(1)} custom-call(f32[128,128]{1,0:T(8,128)S(1)} %convolution_subtract_fusion.36), custom_call_target="Cholesky" | custom-call | tf_op jit(solution)/shard_map/jit(cholesky)/cholesky | solution.py:24
  248.2 7.7 while.11
  255.9 39.3 %custom-call.32 = f32[4,128,128]{1,2,0:T(8,128)S(1)} custom-call(f32[4,128,128]{2,1,0:T(8,128)S(1)} %get-tuple-element.19), custom_call_target="InvertDiagBlocksLowerTriangular" | custom-call | tf_op jit(solution)/shard_map/triangular_solve | solution.py:27
  313.2 4.0 convolution_subtract_fusion.3
  318.6 4.3 convolution_subtract_fusion
  322.9 19.0 %slice_subtract_fusion = f32[1536,1536]{0,1:T(8,128)S(1)} fusion(f32[2048,2048]{0,1:T(8,128)} %convert_element_type.2, f32[1536,128]{1,0:T(8,128)S(1)} %fusion.170, f32[1536,128]{1,0:T(8,128)S(1)} %fusion.168, f32[1536,128]{1,0:T(8,128)S(1)} %fusion.166, f32[1536,128]{1,0:T(8,128)S(1)} %bitcast.243), kind=kOutput, calls=%fused_computation.26 | convolution fusion | flops 14500233216 | bytes 22020096 | tf_op jit(solution)/shard_map/dot_general | solution.py:30
  341.9 3.6 copy-done
  351.9 11.7 %cholesky.534 = f32[128,128]{1,0:T(8,128)S(1)} custom-call(f32[128,128]{1,0:T(8,128)S(1)} %cholesky.759), custom_call_target="Cholesky" | custom-call | tf_op jit(solution)/shard_map/jit(cholesky)/cholesky | solution.py:24
  364.7 9.8 custom-call.50
  377.7 11.7 %cholesky.553 = f32[128,128]{1,0:T(8,128)S(1)} custom-call(f32[128,128]{1,0:T(8,128)S(1)} %cholesky.763), custom_call_target="Cholesky" | custom-call | tf_op jit(solution)/shard_map/jit(cholesky)/cholesky | solution.py:24
  391.4 10.2 custom-call.51
  404.0 11.7 %cholesky.574 = f32[128,128]{1,0:T(8,128)S(1)} custom-call(f32[128,128]{1,0:T(8,128)S(1)} %cholesky.768), custom_call_target="Cholesky" | custom-call | tf_op jit(solution)/shard_map/jit(cholesky)/cholesky | solution.py:24
  417.0 9.8 custom-call.52
  429.1 11.7 %cholesky.591 = f32[128,128]{1,0:T(8,128)S(1)} custom-call(f32[128,128]{1,0:T(8,128)S(1)} %convolution_subtract_fusion.35), custom_call_target="Cholesky" | custom-call | tf_op jit(solution)/shard_map/jit(cholesky)/cholesky | solution.py:24
  447.6 11.7 %while.12 = (s32[]{:T(128)}, f32[512,512]{1,0:T(8,128)}, s32[4,2]{0,1:T(2,128)S(1)}, f32[4,128,128]{2,1,0:T(8,128)S(1)}, s32[]{:T(128)}) while((s32[]{:T(128)}, f32[512,512]{1,0:T(8,128)}, s32[4,2]{0,1:T(2,128)S(1)}, f32[4,128,128]{2,1,0:T(8,128)S(1)}, s32[]{:T(128)}) %tuple.125), condition=%wide.while_cond.2, body=%wide.while_body.2.sunk | while | flops 2 | bytes 131181 | solution.py:27
  459.4 39.3 %custom-call.33 = f32[4,128,128]{1,2,0:T(8,128)S(1)} custom-call(f32[4,128,128]{2,1,0:T(8,128)S(1)} %get-tuple-element.27), custom_call_target="InvertDiagBlocksLowerTriangular" | custom-call | tf_op jit(solution)/shard_map/triangular_solve | solution.py:27
  507.8 3.1 fusion.32
  527.6 9.2 slice_subtract_fusion.1
  545.1 11.7 %cholesky.606 = f32[128,128]{1,0:T(8,128)S(1)} custom-call(f32[128,128]{1,0:T(8,128)S(1)} %cholesky.772), custom_call_target="Cholesky" | custom-call | tf_op jit(solution)/shard_map/jit(cholesky)/cholesky | solution.py:24
  557.9 9.8 custom-call.53
  570.9 11.7 %cholesky.625 = f32[128,128]{1,0:T(8,128)S(1)} custom-call(f32[128,128]{1,0:T(8,128)S(1)} %cholesky.776), custom_call_target="Cholesky" | custom-call | tf_op jit(solution)/shard_map/jit(cholesky)/cholesky | solution.py:24
  584.6 9.9 custom-call.54
  596.9 11.7 %cholesky.646 = f32[128,128]{1,0:T(8,128)S(1)} custom-call(f32[128,128]{1,0:T(8,128)S(1)} %cholesky.781), custom_call_target="Cholesky" | custom-call | tf_op jit(solution)/shard_map/jit(cholesky)/cholesky | solution.py:24
  610.0 9.8 custom-call.55
  622.0 11.7 %cholesky.663 = f32[128,128]{1,0:T(8,128)S(1)} custom-call(f32[128,128]{1,0:T(8,128)S(1)} %convolution_subtract_fusion.34), custom_call_target="Cholesky" | custom-call | tf_op jit(solution)/shard_map/jit(cholesky)/cholesky | solution.py:24
  640.9 11.7 %while.13 = (s32[]{:T(128)}, f32[512,512]{1,0:T(8,128)}, s32[4,2]{0,1:T(2,128)S(1)}, f32[4,128,128]{2,1,0:T(8,128)S(1)}, s32[]{:T(128)}) while((s32[]{:T(128)}, f32[512,512]{1,0:T(8,128)}, s32[4,2]{0,1:T(2,128)S(1)}, f32[4,128,128]{2,1,0:T(8,128)S(1)}, s32[]{:T(128)}) %tuple.126), condition=%wide.while_cond.3, body=%wide.while_body.3.sunk | while | flops 2 | bytes 131181 | solution.py:27
  652.6 39.3 %custom-call.34 = f32[4,128,128]{1,2,0:T(8,128)S(1)} custom-call(f32[4,128,128]{2,1,0:T(8,128)S(1)} %get-tuple-element.35), custom_call_target="InvertDiagBlocksLowerTriangular" | custom-call | tf_op jit(solution)/shard_map/triangular_solve | solution.py:27
  715.7 4.1 convolution_subtract_fusion.5
  725.1 11.8 %cholesky.678 = f32[128,128]{1,0:T(8,128)S(1)} custom-call(f32[128,128]{1,0:T(8,128)S(1)} %cholesky.785), custom_call_target="Cholesky" | custom-call | tf_op jit(solution)/shard_map/jit(cholesky)/cholesky | solution.py:24
  737.0 9.8 custom-call.56
  750.8 11.7 %cholesky.697 = f32[128,128]{1,0:T(8,128)S(1)} custom-call(f32[128,128]{1,0:T(8,128)S(1)} %cholesky.789), custom_call_target="Cholesky" | custom-call | tf_op jit(solution)/shard_map/jit(cholesky)/cholesky | solution.py:24
  765.1 9.8 custom-call.57
  778.2 11.9 %cholesky.718 = f32[128,128]{1,0:T(8,128)S(1)} custom-call(f32[128,128]{1,0:T(8,128)S(1)} %cholesky.794), custom_call_target="Cholesky" | custom-call | tf_op jit(solution)/shard_map/jit(cholesky)/cholesky | solution.py:24
  791.5 9.8 custom-call.58
  803.6 11.7 %cholesky.735 = f32[128,128]{1,0:T(8,128)S(1)} custom-call(f32[128,128]{1,0:T(8,128)S(1)} %convolution_subtract_fusion.33), custom_call_target="Cholesky" | custom-call | tf_op jit(solution)/shard_map/jit(cholesky)/cholesky | solution.py:24
  822.6 13.6 %while.14 = (s32[]{:T(128)}, f32[512,512]{1,0:T(8,128)}, s32[4,2]{0,1:T(2,128)S(1)}, f32[4,128,128]{2,1,0:T(8,128)}, s32[]{:T(128)}) while((s32[]{:T(128)}, f32[512,512]{1,0:T(8,128)}, s32[4,2]{0,1:T(2,128)S(1)}, f32[4,128,128]{2,1,0:T(8,128)}, s32[]{:T(128)}) %tuple.127), condition=%wide.while_cond.clone.2, body=%wide.while_body.clone.2.sunk | while | flops 2 | bytes 132705 | solution.py:47
  836.2 41.0 %custom-call.62 = f32[4,128,128]{1,2,0:T(8,128)} custom-call(f32[4,128,128]{2,1,0:T(8,128)} %get-tuple-element.57), custom_call_target="InvertDiagBlocksLowerTriangular" | custom-call | tf_op jit(solution)/shard_map/triangular_solve/custom-call.10 | solution.py:47
  891.7 5.4 fusion.9
  897.2 128.3 %all-gather.5.cloned.1.call-done = bf16[2048,2048]{1,0:T(8,128)(2,1)} async-done(((bf16[2048,256]{1,0:T(8,128)(2,1)}), bf16[2048,2048]{1,0:T(8,128)(2,1)}) %all-gather.5.cloned.1.call-update) | async-done | bytes 8388624 | tf_op jit(solution)/shard_map/all_gather | solution.py:74
  1025.5 7.9 convolution_subtract_fusion.1
  (289 shorter events, 211.5 us)
Async XLA Ops:
  7.2 2.5 copy-start.30
  7.2 131.1 %all-gather.3.cloned.1.call-start = ((), (), s32[]{:S(2)}) async-start(), calls=%async_computation | async-start | bytes 9437184 | tf_op jit(solution)/shard_map/all_gather | solution.py:68
  9.6 1015.9 %all-gather.5.cloned.1.call-start = ((), (), s32[]{:S(2)}) async-start(), calls=%async_computation.1 | async-start | bytes 9437184 | tf_op jit(solution)/shard_map/all_gather | solution.py:74
  255.9 53.0 %copy-start.11 = (f32[512,512]{1,0:T(8,128)}, f32[512,512]{1,0:T(8,128)S(1)}, u32[]{:S(2)}) copy-start(f32[512,512]{1,0:T(8,128)S(1)} %get-tuple-element.334) | copy-start | bytes 3145732
  295.3 1.6 copy-start.28
  299.1 7.3 copy-start.29
  313.2 5.4 copy-start.14
  318.6 4.3 copy-start.2
  341.9 3.6 copy-start
  350.9 1.0 copy-start.16
  498.7 1.8 copy-start.24
  506.9 0.8 copy-start.10
  515.0 7.7 copy-start.25
  515.0 8.7 copy-start.23
  518.7 6.1 copy-start.3
  518.7 6.1 copy-start.4
  518.7 6.1 copy-start.6
  518.7 6.1 copy-start.37
  524.8 2.8 copy-start.8
  536.8 1.9 copy-start.1
  544.1 1.0 copy-start.17
  691.9 1.5 copy-start.26
  698.8 0.7 copy-start.22
  704.7 11.1 %copy-start.20 = (f32[512,128]{1,0:T(8,128)}, f32[512,128]{1,0:T(8,128)S(1)}, u32[]{:S(2)}) copy-start(f32[512,128]{1,0:T(8,128)S(1)} %copy.22) | copy-start | bytes 786436
  704.7 6.3 copy-start.36
  704.7 7.6 copy-start.27
  704.7 8.6 copy-start.31
  706.1 7.8 copy-start.18
  706.1 7.8 copy-start.19
  713.9 1.8 copy-start.21
  724.1 1.0 copy-start.15
  749.7 1.1 copy-start.35
  836.2 49.7 %copy-start.32 = (bf16[512,256]{1,0:T(8,128)(2,1)S(1)}, bf16[512,256]{1,0:T(8,128)(2,1)}, u32[]{:S(2)}) copy-start(bf16[512,256]{1,0:T(8,128)(2,1)} %fusion.80) | copy-start | bytes 786436
  836.2 49.7 %copy-start.33 = (bf16[512,256]{1,0:T(8,128)(2,1)S(1)}, bf16[512,256]{1,0:T(8,128)(2,1)}, u32[]{:S(2)}) copy-start(bf16[512,256]{1,0:T(8,128)(2,1)} %fusion.79) | copy-start | bytes 786436
  877.2 8.7 copy-start.34
  886.0 3.7 collective-permute-start
  889.7 1.0 copy-start.5
  889.7 1.2 copy-start.7
  889.7 1.3 copy-start.9
  889.7 1.7 copy-start.12
  889.7 2.0 copy-start.13
Sparse Core Ops, SparseCore 0:
  10.6 127.6 all-gather.2
  889.8 135.6 all-gather.4
where the time goes:
time: 1050 us; the launch traced here: 1040 us
  other arithmetic  530 us (50%)
  waiting for transfers between devices  256 us (24%)
  matrix products  143 us (14%)
  local copies, waits for them, and re-layouts  82.9 us (8%)
  between operations  25.7 us (2%)
    another operation x59, other arithmetic, blocked_cholesky(): head_lower = jnp.linalg.cholesky(head)  334 us
    all_gather x1, waiting for transfers between devices, local(): lax.all_gather(arrived, 'blk', axis=1, tiled=True)  128 us
    all_gather x1, waiting for transfers between devices, local(): lax.all_gather(schur, 'blk', axis=0, tiled=True).astype(jnp.float32)  127 us
    another operation x7, other arithmetic, blocked_cholesky(): lax.linalg.triangular_solve(head_lower, below, left_side=False, lower=Tru...  125 us
    another operation x2, other arithmetic, blocked_forward(): lax.linalg.triangular_solve(head_lower, remaining[:width], left_side=True...  43.8 us
    another operation x21, matrix products, blocked_cholesky(): lax.linalg.triangular_solve(head_lower, below, left_side=False, lower=Tru...  36.7 us
    dot_general x3, matrix products, blocked_cholesky(): jnp.dot(below_lower, below_lower.T, precision=lax.Precision.HIGHEST)  32.2 us
    another operation x28, matrix products, blocked_forward(): lax.linalg.triangular_solve(head_lower, remaining[:width], left_side=True...  31.8 us
  transfers between devices with their start and end apart: 3, of which 3 were waited for; matrix products, arithmetic and copies ran while one was open for 1% of the time, Pallas kernels for 0%

commit v1 on v0

v1 whole, which is shorter than its diff:
```python
import functools
import jax
import jax.numpy as jnp
from jax import lax
from jax.experimental import pallas as pl
from jax.experimental.pallas import tpu as pltpu

B = 128
BF = jnp.bfloat16
F32 = jnp.float32


def split(x):
    hi = x.astype(BF)
    return hi, (x - hi.astype(F32)).astype(BF)


def dot_t(a, b):
    return lax.dot_general(a, b, (((1,), (1,)), ((), ())), preferred_element_type=F32)


def eliminate(block):
    size = block.shape[0]
    count = size // 8
    sub = lax.broadcasted_iota(jnp.int32, (8, size), 0)
    lane = lax.broadcasted_iota(jnp.int32, (8, size), 1)
    rows = [block[8 * t : 8 * t + 8, :] for t in range(count)]
    inv = [jnp.where(lane == sub + 8 * t, 1.0, 0.0).astype(F32) for t in range(count)]
    for k in range(size):
        s, r = divmod(k, 8)
        row_a = jnp.broadcast_to(rows[s][r : r + 1, :], (8, size))
        row_n = jnp.broadcast_to(inv[s][r : r + 1, :], (8, size))
        pivot = jnp.broadcast_to(row_a[:, k : k + 1], (8, size))
        scale = lax.rsqrt(pivot)
        u_a = row_a * scale
        u_n = row_n * scale
        w_a = u_a * scale
        w_n = u_n * scale
        for t in range(s, count):
            c = jnp.broadcast_to(rows[t][:, k : k + 1], (8, size))
            if t == s:
                keep = sub > r
                c = jnp.where(keep, c, 0.0)
                here = sub == r
                rows[t] = jnp.where(here, u_a, rows[t] - c * w_a)
                inv[t] = jnp.where(here, u_n, inv[t] - c * w_n)
            else:
                rows[t] = rows[t] - c * w_a
                inv[t] = inv[t] - c * w_n
    return jnp.concatenate(rows, 0), jnp.concatenate(inv, 0)


def factor_kernel(total, s_ref, c_ref, f_ref, y_ref, work, left, right):
    extra = c_ref.shape[0]
    panels = total // B
    T = 256
    me = lax.axis_index("blk")

    def load(i, _):
        at = pl.multiple_of(i * T, T)
        work[pl.ds(at, T), :] = s_ref[pl.ds(at, T), :].astype(F32)
        return 0

    lax.fori_loop(0, total // T, load, 0)
    work[pl.ds(total, extra), :] = c_ref[...].astype(F32)
    f_ref[...] = jnp.zeros_like(f_ref)
    tri = lax.broadcasted_iota(jnp.int32, (B, B), 0) >= lax.broadcasted_iota(jnp.int32, (B, B), 1)

    def panel(p, _):
        at = pl.multiple_of(p * B, B)
        col = pl.ds(at, B)
        upper, inv = eliminate(work[col, col])
        ih, il = split(inv)
        first = p * B // T
        inv3 = jnp.concatenate([ih, il, ih], 1)

        def solve(i, _):
            rr = pl.ds(pl.multiple_of(i * T, T), T)
            bh, bl = split(work[rr, col])
            x = dot_t(jnp.concatenate([bh, bh, bl], 1), inv3)
            work[rr, col] = x
            xh, xl = split(x)
            left[rr, :] = jnp.concatenate([xh, xh, xl], 1)
            right[rr, :] = jnp.concatenate([xh, xl, xh], 1)
            return 0

        lax.fori_loop(first, (total + extra) // T, solve, 0)
        work[col, col] = jnp.where(tri, upper.T, 0.0)

        def update_col(j, _):
            cc = pl.ds(pl.multiple_of(j * T, T), T)
            b = right[cc, :]

            def update(i, _):
                rr = pl.ds(pl.multiple_of(i * T, T), T)
                work[rr, cc] = work[rr, cc] - dot_t(left[rr, :], b)
                return 0

            lax.fori_loop(j, (total + extra) // T, update, 0)
            return 0

        if True:
            @pl.when(p % 2 == 0)
            def _():
                half = pl.ds(pl.multiple_of(at + B, B), B)
                b = right[half, :]

                def update(i, _):
                    rr = pl.ds(pl.multiple_of(i * T, T), T)
                    work[rr, half] = work[rr, half] - dot_t(left[rr, :], b)
                    return 0

                lax.fori_loop(first, (total + extra) // T, update, 0)

        lax.fori_loop(first + 1, total // T, update_col, 0)
        return 0

    lax.fori_loop(0, panels, panel, 0)
    f_ref[...] = work[pl.ds(pl.multiple_of(me * extra, extra), extra), :]
    for q in range(total // B):
        @pl.when(q * B >= (me + 1) * extra)
        def _():
            f_ref[:, q * B : (q + 1) * B] = jnp.zeros((extra, B), F32)
        if True:
            rowi = me * extra + lax.broadcasted_iota(jnp.int32, (extra, B), 0)
            coli = q * B + lax.broadcasted_iota(jnp.int32, (extra, B), 1)
            f_ref[:, q * B : (q + 1) * B] = jnp.where(rowi >= coli, f_ref[:, q * B : (q + 1) * B], 0.0)
    y_ref[...] = work[pl.ds(total, extra), :].astype(BF)


def factor_call(s, c):
    total, extra = s.shape[1], c.shape[0]
    return pl.pallas_call(
        functools.partial(factor_kernel, total),
        out_shape=(jax.ShapeDtypeStruct((extra, total), F32), jax.ShapeDtypeStruct((extra, total), BF)),
        in_specs=[pl.BlockSpec(memory_space=pltpu.VMEM)] * 2,
        out_specs=(pl.BlockSpec(memory_space=pltpu.VMEM), pl.BlockSpec(memory_space=pltpu.VMEM)),
        scratch_shapes=[
            pltpu.VMEM((total + extra, total), F32),
            pltpu.VMEM((total + extra, 3 * B), BF),
            pltpu.VMEM((total + extra, 3 * B), BF),
        ],
        compiler_params=pltpu.CompilerParams(vmem_limit_bytes=60 * 1024 * 1024),
        name="factor_slab",
    )(s, c)
from jax.sharding import PartitionSpec as P


def passed_along(value, axis, steps):
    count = lax.axis_size(axis)
    initial, last = (max(0, -steps), min(count, count - steps))
    return lax.ppermute(value, axis, [(source, source + steps) for source in range(initial, last)])


def local(schur, coupling, next_diag):
    whole = lax.all_gather(schur, "blk", axis=0, tiled=True)
    my_rows, solved = factor_call(whole, coupling)
    arrived = passed_along(solved, "chain", 1)
    every = lax.all_gather(arrived, "blk", axis=0, tiled=True)
    return (my_rows, next_diag - dot_t(arrived, every))


def solution(mesh):
    placed = (P(("chain", "blk"), None),) * 3
    return jax.shard_map(
        local, mesh=mesh, in_specs=placed, out_specs=(P(("chain", "blk"), None),) * 2, check_vma=False
    )
```

time: 1050 us -> 667 us (0.64)
  other arithmetic: 530 us -> 0 us
  Pallas kernels: 0 us -> 375 us
  matrix products: 143 us -> 7.4 us
  local copies, waits for them, and re-layouts: 82.9 us -> 1.06 us
  waiting for transfers between devices: 256 us -> 268 us
  between operations: 25.7 us -> 14.1 us
    another operation x72 -> x0, other arithmetic: 505 us -> none  [the longest x59 334 us: blocked_cholesky(): head_lower = jnp.linalg.cholesky(head)]
    pallas_call x0 -> x1, Pallas kernels: none -> 375 us  [factor_call(): pl.pallas_call(functools.partial(factor_kernel, total), out_shape=(jax.Sh...]
    another operation x73 -> x0, matrix products: 94.2 us -> none  [the longest x21 36.7 us: blocked_cholesky(): lax.linalg.triangular_solve(head_lower, below, left_side=False, lower=Tru...]
    another operation x75 -> x0, local copies, waits for them, and re-layouts: 56.1 us -> none
    dot_general x7 -> x1, matrix products: 49 us -> 7.4 us  [dot_t(): lax.dot_general(a, b, (((1,), (1,)), ((), ())), preferred_element_type=F32)]
    unnamed x82 -> x4, local copies, waits for them, and re-layouts: 15.3 us -> 1.06 us
    convert_element_type x1 -> x0, other arithmetic: 11.2 us -> none  [local(): lax.all_gather(schur, 'blk', axis=0, tiled=True).astype(jnp.float32)]
  transfers between devices with their start and end apart: 3 -> 3, of which waited for: 3 -> 3; matrix products, arithmetic and copies ran while one was open for 1% -> 0% of each run, Pallas kernels for 0% -> 0%
where the time goes in v1:
time: 667 us
  Pallas kernels  375 us (56%)
  waiting for transfers between devices  268 us (40%)
  between operations  14.1 us (2%)
  matrix products  7.4 us (1%)
    pallas_call x1, Pallas kernels, factor_call(): pl.pallas_call(functools.partial(factor_kernel, total), out_shape=(jax.Sh...  375 us
    all_gather x1, waiting for transfers between devices, local(): every = lax.all_gather(arrived, 'blk', axis=0, tiled=True)  135 us
    all_gather x1, waiting for transfers between devices, local(): whole = lax.all_gather(schur, 'blk', axis=0, tiled=True)  129 us
  transfers between devices with their start and end apart: 3, of which 3 were waited for; matrix products, arithmetic and copies ran while one was open for 0% of the time, Pallas kernels for 0%

profile of v1, /device:TPU:0, one launch (start us, length us, event | category | flops | bytes accessed | tf_op | source)
XLA Modules:
  0.0 667.2 jit_solution(15727027125865085324)
XLA Ops:
  7.2 0.0 all-gather.3.cloned.1.call-start
  7.2 0.7 all-gather.3.cloned.1.call-update
  7.9 0.0 copy-start.1
  7.9 0.0 all-gather.5.cloned.1.call-start
  8.0 129.4 %all-gather.3.cloned.1.call-done.s_ref = bf16[2048,2048]{1,0:T(8,128)(2,1)} async-done(((bf16[256,2048]{1,0:T(8,128)(2,1)}), bf16[2048,2048]{1,0:T(8,128)(2,1)}) %all-gather.3.cloned.1.call-update) | async-done | bytes 8388624 | tf_op jit(solution)/shard_map/all_gather | solution.py:156
  137.3 375.5 %factor_slab.1 = (f32[256,2048]{1,0:T(8,128)}, bf16[256,2048]{1,0:T(8,128)(2,1)}) custom-call(bf16[2048,2048]{1,0:T(8,128)(2,1)} %all-gather.3.cloned.1.call-done.s_ref, bf16[256,2048]{1,0:T(8,128)(2,1)} %c_ref.1), custom_call_target="tpu_custom_call" | custom-call | tf_op jit(solution)/shard_map/factor_slab/pallas_call | solution.py:133
  512.8 1.3 collective-permute-start
  514.2 2.4 collective-permute-done
  516.6 0.0 copy-start
  516.6 1.1 copy-done
  517.6 0.0 all-gather.5.cloned.1.call-update
  517.7 135.3 %all-gather.5.cloned.1.call-done = bf16[2048,2048]{1,0:T(8,128)(2,1)} async-done(((bf16[256,2048]{1,0:T(8,128)(2,1)}), bf16[2048,2048]{1,0:T(8,128)(2,1)}) %all-gather.5.cloned.1.call-update) | async-done | bytes 8388624 | tf_op jit(solution)/shard_map/all_gather | solution.py:159
  652.9 0.0 copy-done.1
  652.9 7.4 %convolution_subtract_fusion = f32[256,2048]{1,0:T(8,128)} fusion(f32[256,2048]{1,0:T(8,128)S(1)} %copy-done.1, bf16[256,2048]{1,0:T(8,128)(2,1)} %copy-done, bf16[2048,2048]{1,0:T(8,128)(2,1)} %all-gather.5.cloned.1.call-done), kind=kOutput, calls=%fused_computation | convolution fusion | flops 2148007936 | bytes 13631488 | tf_op jit(solution)/shard_map/dot_general | solution.py:19
Async XLA Ops:
  7.2 130.2 %all-gather.3.cloned.1.call-start = ((), (), s32[]{:S(2)}) async-start(), calls=%async_computation | async-start | bytes 9437184 | tf_op jit(solution)/shard_map/all_gather | solution.py:156
  7.9 645.0 %copy-start.1 = (f32[256,2048]{1,0:T(8,128)S(1)}, f32[256,2048]{1,0:T(8,128)}, u32[]{:S(2)}) copy-start(f32[256,2048]{1,0:T(8,128)} %param.5) | copy-start | bytes 6291460
  7.9 645.0 %all-gather.5.cloned.1.call-start = ((), (), s32[]{:S(2)}) async-start(), calls=%async_computation.1 | async-start | bytes 9437184 | tf_op jit(solution)/shard_map/all_gather | solution.py:159
  512.8 3.8 collective-permute-start
  516.6 1.1 copy-start
Sparse Core Ops, SparseCore 0:
  10.1 127.1 all-gather.2
  517.8 135.0 all-gather.4

commit v2 on v1

v2 whole, which is shorter than its diff:
```python
import functools
import jax
import jax.numpy as jnp
from jax import lax
from jax.experimental import pallas as pl
from jax.experimental.pallas import tpu as pltpu
from jax.sharding import PartitionSpec as P

B = 128
BF = jnp.bfloat16
F32 = jnp.float32


def split(x):
    hi = x.astype(BF)
    return hi, (x - hi.astype(F32)).astype(BF)


def dot_t(a, b):
    return lax.dot_general(a, b, (((1,), (1,)), ((), ())), preferred_element_type=F32)


def eliminate(block):
    size = block.shape[0]
    count = size // 8
    sub = lax.broadcasted_iota(jnp.int32, (8, size), 0)
    lane = lax.broadcasted_iota(jnp.int32, (8, size), 1)
    rows = [block[8 * t : 8 * t + 8, :] for t in range(count)]
    inv = [jnp.where(lane == sub + 8 * t, 1.0, 0.0).astype(F32) for t in range(count)]
    group = 4

    def lane_of(x, k):
        return jnp.broadcast_to(x[:, k : k + 1], (8, size))

    def row_of(x, r):
        return jnp.broadcast_to(x[r : r + 1, :], (8, size))

    for k in range(0, size, group):
        s, r = divmod(k, 8)
        span = range(group)
        u = [row_of(rows[s], r + i) for i in span]
        n = [row_of(inv[s], r + i) for i in span]
        pivot = [[lane_of(u[i], k + j) if j >= i else None for j in span] for i in span]
        scale = [None] * group
        for i in span:
            scale[i] = lax.rsqrt(pivot[i][i])
            u[i] = u[i] * scale[i]
            n[i] = n[i] * scale[i]
            for j in range(i + 1, group):
                pivot[i][j] = pivot[i][j] * scale[i]
            for j in range(i + 1, group):
                u[j] = u[j] - pivot[i][j] * u[i]
                n[j] = n[j] - pivot[i][j] * n[i]
                for m in range(j, group):
                    pivot[j][m] = pivot[j][m] - pivot[i][j] * pivot[i][m]
        for t in range(s, count):
            if t == s and r + group == 8:
                new_a, new_n = rows[t], inv[t]
            else:
                c = [lane_of(rows[t], k + i) for i in span]
                new_a, new_n = rows[t], inv[t]
                for i in span:
                    x = c[i] * scale[i]
                    for j in range(i + 1, group):
                        c[j] = c[j] - x * pivot[i][j]
                    if t == s:
                        x = jnp.where(sub >= r + group, x, 0.0)
                    new_a = new_a - x * u[i]
                    new_n = new_n - x * n[i]
            if t == s:
                for i in span:
                    new_a = jnp.where(sub == r + i, u[i], new_a)
                    new_n = jnp.where(sub == r + i, n[i], new_n)
            rows[t], inv[t] = new_a, new_n
    return jnp.concatenate(rows, 0), jnp.concatenate(inv, 0)


def chunk_kernel(total, start, s_ref, c_ref, *refs):
    priors = refs[:-6]
    x_ref, f_ref, y_ref, work, left, right = refs[-6:]
    extra, width = c_ref.shape
    T = 2 * B
    me = lax.axis_index("blk")
    tail = pl.ds(total, extra)
    own = pl.ds(start, width)

    def tile(i):
        return pl.ds(pl.multiple_of(i * T, T), T)

    def over_rows(first, visit):
        def step(i, _):
            visit(tile(i))
            return 0

        lax.fori_loop(first, total // T, step, 0)
        visit(tail)

    def bring(rr, value):
        for prior in priors:
            hi, lo = prior[rr, :width], prior[rr, width:]
            own_hi, own_lo = prior[own, :width], prior[own, width:]
            value = value - (dot_t(hi, own_hi) + (dot_t(hi, own_lo) + dot_t(lo, own_hi)))
        work[rr, :] = value

    def load(i, _):
        bring(tile(i), s_ref[tile(i), :].astype(F32))
        return 0

    lax.fori_loop(start // T, total // T, load, 0)
    bring(tail, c_ref[...].astype(F32))
    tri = lax.broadcasted_iota(jnp.int32, (B, B), 0) >= lax.broadcasted_iota(jnp.int32, (B, B), 1)

    def panel(p, _):
        at = pl.multiple_of(p * B, B)
        here = pl.ds(pl.multiple_of(start + at, B), B)
        col = pl.ds(at, B)
        low_col = pl.ds(pl.multiple_of(width + at, B), B)
        slot = pl.ds(pl.multiple_of((p % 2) * 3 * B, 3 * B), 3 * B)
        upper, inv = eliminate(work[here, col])
        ih, il = split(inv)
        inv3 = jnp.concatenate([ih, il, ih], 1)
        first = start // T + p // 2

        def solve(rr):
            bh, bl = split(work[rr, col])
            x = dot_t(jnp.concatenate([bh, bh, bl], 1), inv3)
            work[rr, col] = x
            xh, xl = split(x)
            left[rr, slot] = jnp.concatenate([xh, xh, xl], 1)
            right[rr, slot] = jnp.concatenate([xh, xl, xh], 1)
            x_ref[rr, col] = xh
            x_ref[rr, low_col] = xl

        over_rows(first, solve)
        work[here, col] = jnp.where(tri, upper.T, 0.0)

        @pl.when(p % 2 == 0)
        def _():
            half = pl.ds(pl.multiple_of(at + B, B), B)
            b = right[pl.ds(pl.multiple_of(start + at + B, B), B), : 3 * B]

            def update(rr):
                work[rr, half] = work[rr, half] - dot_t(left[rr, : 3 * B], b)

            over_rows(first, update)

        @pl.when(p % 2 == 1)
        def _():
            def update_col(j, _):
                b = right[pl.ds(pl.multiple_of(start + j * T, T), T), :]

                def update(rr):
                    work[rr, tile(j)] = work[rr, tile(j)] - dot_t(left[rr, :], b)

                over_rows(start // T + j, update)
                return 0

            lax.fori_loop(p // 2 + 1, width // T, update_col, 0)

        return 0

    lax.fori_loop(0, width // B, panel, 0)
    row = me * extra + lax.broadcasted_iota(jnp.int32, (extra, width), 0)
    column = start + lax.broadcasted_iota(jnp.int32, (extra, width), 1)
    mine = work[pl.ds(pl.multiple_of(me * extra, extra), extra), :]
    f_ref[...] = jnp.where(row >= column, mine, 0.0)
    y_ref[...] = work[tail, :].astype(BF)


def chunk_call(start, s, c, priors):
    total, (extra, width) = s.shape[0], c.shape
    every = total + extra
    live = every - start
    vmem = pl.BlockSpec(memory_space=pltpu.VMEM)
    return pl.pallas_call(
        functools.partial(chunk_kernel, total, start),
        out_shape=(
            jax.ShapeDtypeStruct((every, 2 * width), BF),
            jax.ShapeDtypeStruct((extra, width), F32),
            jax.ShapeDtypeStruct((extra, width), BF),
        ),
        in_specs=[vmem] * (2 + len(priors)),
        out_specs=(vmem, vmem, vmem),
        scratch_shapes=[
            pltpu.VMEM((every, width), F32),
            pltpu.VMEM((every, 6 * B), BF),
            pltpu.VMEM((every, 6 * B), BF),
        ],
        compiler_params=pltpu.CompilerParams(vmem_limit_bytes=56 * 1024 * 1024),
        cost_estimate=pl.CostEstimate(flops=COST, bytes_accessed=8 * live * width, transcendentals=0),
        name="factor_chunk",
    )(s, c, *priors)


COST = 50000000000


def passed_along(value, axis, steps):
    count = lax.axis_size(axis)
    initial, last = (max(0, -steps), min(count, count - steps))
    return lax.ppermute(value, axis, [(source, source + steps) for source in range(initial, last)])


def local(schur, coupling, next_diag):
    total = schur.shape[1]
    width = max(total // 4, 2 * B)
    starts = range(0, total, width)
    early = lax.all_gather(schur[:, :width], "blk", axis=0, tiled=True)
    late = lax.all_gather(schur[:, width:], "blk", axis=0, tiled=True)
    wholes = [early] + [late[:, at - width : at] for at in starts[1:]]
    priors, factors = [], []
    fresh, waiting = next_diag, None
    for at, whole in zip(starts, wholes):
        held, rows, solved = chunk_call(at, whole, coupling[:, at : at + width], priors)
        priors.append(held)
        factors.append(rows)
        arrived = passed_along(solved, "chain", 1)
        priors, arrived = lax.optimization_barrier((priors, arrived))
        if waiting is not None:
            fresh = fresh - dot_t(*waiting)
            priors, fresh = lax.optimization_barrier((priors, fresh))
        waiting = (arrived, lax.all_gather(arrived, "blk", axis=0, tiled=True))
    fresh = fresh - dot_t(*waiting)
    return (jnp.concatenate(factors, axis=1), fresh)


def solution(mesh):
    placed = (P(("chain", "blk"), None),) * 3
    return jax.shard_map(
        local, mesh=mesh, in_specs=placed, out_specs=(P(("chain", "blk"), None),) * 2, check_vma=False
    )
```

time: 667 us -> 382 us (0.57)
  Pallas kernels: 375 us -> 168 us
  waiting for transfers between devices: 268 us -> 156 us
  local copies, waits for them, and re-layouts: 1.06 us -> 13.4 us
  starting transfers between devices: 1.42 us -> 12.3 us
  matrix products: 7.4 us -> 14.6 us
    pallas_call x1 -> x4, Pallas kernels: 375 us -> 168 us  [chunk_call(): pl.pallas_call(functools.partial(chunk_kernel, total, start), out_shape=(...]
    all_gather x2 -> x6, waiting for transfers between devices: 265 us -> 152 us  [the longest x1 54.8 us: local(): late = lax.all_gather(schur[:, width:], 'blk', axis=0, tiled=True)]
    ppermute x1 -> x4, starting transfers between devices: 1.34 us -> 11.9 us  [passed_along(): lax.ppermute(value, axis, [(source, source + steps) for source in range(i...]
    slice x0 -> x4, local copies, waits for them, and re-layouts: none -> 10.5 us  [the longest x1 5.71 us: local(): wholes = [early] + [late[:, at - width:at] for at in starts[1:]]]
    dot_general x1 -> x4, matrix products: 7.4 us -> 14.6 us  [dot_t(): lax.dot_general(a, b, (((1,), (1,)), ((), ())), preferred_element_type=F32)]
  transfers between devices with their start and end apart: 3 -> 10, of which waited for: 3 -> 7; matrix products, arithmetic and copies ran while one was open for 0% -> 6% of each run, Pallas kernels for 0% -> 44%
where the time goes in v2:
time: 382 us; the launch traced here: 381 us
  Pallas kernels  168 us (44%)
  waiting for transfers between devices  156 us (41%)
  matrix products  14.6 us (4%)
  between operations  14.2 us (4%)
  local copies, waits for them, and re-layouts  13.4 us (4%)
  starting transfers between devices  12.3 us (3%)
    pallas_call x4, Pallas kernels, chunk_call(): pl.pallas_call(functools.partial(chunk_kernel, total, start), out_shape=(...  168 us
    all_gather x1, waiting for transfers between devices, local(): late = lax.all_gather(schur[:, width:], 'blk', axis=0, tiled=True)  54.8 us
    all_gather x1, waiting for transfers between devices, local(): early = lax.all_gather(schur[:, :width], 'blk', axis=0, tiled=True)  49.8 us
    all_gather x4, waiting for transfers between devices, local(): waiting = (arrived, lax.all_gather(arrived, 'blk', axis=0, tiled=True))  47.6 us
    dot_general x4, matrix products, dot_t(): lax.dot_general(a, b, (((1,), (1,)), ((), ())), preferred_element_type=F32)  14.6 us
    ppermute x4, starting transfers between devices, passed_along(): lax.ppermute(value, axis, [(source, source + steps) for source in range(i...  11.9 us
  transfers between devices with their start and end apart: 10, of which 7 were waited for; matrix products, arithmetic and copies ran while one was open for 6% of the time, Pallas kernels for 44%

profile of v2, /device:TPU:0, one launch (start us, length us, event | category | flops | bytes accessed | tf_op | source)
XLA Modules:
  0.0 381.4 jit_solution(802488639216754284)
XLA Ops:
  7.2 0.0 copy-start.9
  7.2 0.0 all-gather.7.cloned.1.call-start
  7.2 1.8 slice.27
  9.0 0.0 all-gather.7.cloned.1.call-update
  9.0 0.0 all-gather.9.cloned.1.call-start
  9.0 2.1 slice.29
  11.1 0.0 all-gather.9.cloned.1.call-update
  11.1 0.0 all-gather.11.cloned.1.call-start
  11.2 0.0 copy-done.9
  11.2 1.0 fusion.1
  12.2 49.8 %all-gather.7.cloned.1.call-done.s_ref = bf16[2048,512]{1,0:T(8,128)(2,1)} async-done(((bf16[256,512]{1,0:T(8,128)(2,1)}), bf16[2048,512]{1,0:T(8,128)(2,1)}) %all-gather.7.cloned.1.call-update) | async-done | bytes 2097168 | tf_op jit(solution)/shard_map/all_gather | solution.py:208
  61.9 41.9 %factor_chunk.4 = (bf16[2304,1024]{1,0:T(8,128)(2,1)}, f32[256,512]{1,0:T(8,128)}, bf16[256,512]{1,0:T(8,128)(2,1)}) custom-call(bf16[2048,512]{1,0:T(8,128)(2,1)} %all-gather.7.cloned.1.call-done.s_ref, bf16[256,512]{1,0:T(8,128)(2,1)} %get-tuple-element.63.c_ref), custom_call_target="tpu_custom_call" | custom-call | flops 49999998976 | bytes 9437184 | tf_op jit(solution)/shard_map/factor_chunk/pallas_call | solution.py:175
  103.8 1.3 collective-permute-start
  105.1 1.3 collective-permute-done
  106.5 0.7 copy-done.5
  107.2 0.0 all-gather.11.cloned.1.call-update
  107.2 0.0 all-gather.13.cloned.1.call-start
  107.2 54.8 %all-gather.9.cloned.1.call-done = bf16[2048,1536]{1,0:T(8,128)(2,1)} async-done(((bf16[256,1536]{1,0:T(8,128)(2,1)}), bf16[2048,1536]{1,0:T(8,128)(2,1)}) %all-gather.9.cloned.1.call-update) | async-done | bytes 6291472 | tf_op jit(solution)/shard_map/all_gather | solution.py:209
  162.0 5.7 %fusion = (bf16[2048,512]{1,0:T(8,128)(2,1)}, bf16[2048,512]{1,0:T(8,128)(2,1)}, bf16[2048,512]{1,0:T(8,128)(2,1)}) fusion(bf16[2048,1536]{1,0:T(8,128)(2,1)} %all-gather.9.cloned.1.call-done), kind=kLoop, calls=%fused_computation.5 | loop fusion | bytes 12582912 | tf_op jit(solution)/shard_map/slice | solution.py:210
  167.7 44.0 %factor_chunk.5 = (bf16[2304,1024]{1,0:T(8,128)(2,1)}, f32[256,512]{1,0:T(8,128)}, bf16[256,512]{1,0:T(8,128)(2,1)}) custom-call(bf16[2048,512]{1,0:T(8,128)(2,1)} %get-tuple-element.60.s_ref, bf16[256,512]{1,0:T(8,128)(2,1)} %get-tuple-element.62.c_ref, bf16[2304,1024]{1,0:T(8,128)(2,1)} %get-tuple-element.50.refs_0_), custom_call_target="tpu_custom_call" | custom-call | flops 49999998976 | bytes 7340032 | tf_op jit(solution)/shard_map/factor_chunk/pallas_call | solution.py:175
  211.7 1.3 collective-permute-start.1
  213.0 0.0 all-gather.11.cloned.1.call-done
  213.0 0.0 copy-done
  213.0 0.0 copy-done.6
  213.1 3.7 convolution_subtract_fusion.3
  216.7 0.0 collective-permute-done.1
  216.7 0.7 copy-done.3
  217.4 0.0 all-gather.13.cloned.1.call-update
  217.5 0.2 all-gather.15.cloned.1.call-start
  217.7 0.0 copy-start.4
  217.7 42.4 %factor_chunk.6 = (bf16[2304,1024]{1,0:T(8,128)(2,1)}, f32[256,512]{1,0:T(8,128)}, bf16[256,512]{1,0:T(8,128)(2,1)}) custom-call(bf16[2048,512]{1,0:T(8,128)(2,1)} %get-tuple-element.58.s_ref, bf16[256,512]{1,0:T(8,128)(2,1)} %get-tuple-element.61.c_ref, bf16[2304,1024]{1,0:T(8,128)(2,1)} %get-tuple-element.50.refs_0_, ...), custom_call_target="tpu_custom_call" | custom-call | flops 49999998976 | bytes 5242880 | tf_op jit(solution)/shard_map/factor_chunk/pallas_call | solution.py:175
  260.1 4.0 %collective-permute-start.2 = (bf16[256,512]{1,0:T(8,128)(2,1)}, bf16[256,512]{1,0:T(8,128)(2,1)S(1)}, u32[]{:S(2)}, u32[]{:S(2)}) collective-permute-start(bf16[256,512]{1,0:T(8,128)(2,1)} %get-tuple-element.44), channel_id=1, source_target_pairs={{0,8},{8,16},{16,24},{1,9},{9,17},{17,25},{2,10},{10,18},{18,26},{... | collective-permute-start | bytes 786440 | tf_op jit(solution)/shard_map/ppermute | solution.py:201
  264.1 1.3 collective-permute-done.2
  265.4 0.7 copy-done.1
  266.1 0.0 all-gather.15.cloned.1.call-update
  266.2 0.0 all-gather.17.cloned.1.call-start
  266.2 1.5 all-gather.13.cloned.1.call-done
  267.7 3.0 convolution_subtract_fusion.2
  270.7 39.5 %factor_chunk.7 = (bf16[2304,1024]{1,0:T(8,128)(2,1)}, f32[256,512]{1,0:T(8,128)}, bf16[256,512]{1,0:T(8,128)(2,1)}) custom-call(bf16[2048,512]{1,0:T(8,128)(2,1)} %get-tuple-element.59.s_ref, bf16[256,512]{1,0:T(8,128)(2,1)} %get-tuple-element.64.c_ref, bf16[2304,1024]{1,0:T(8,128)(2,1)} %get-tuple-element.50.refs_0_, ...), custom_call_target="tpu_custom_call" | custom-call | flops 49999998976 | bytes 3145728 | tf_op jit(solution)/shard_map/factor_chunk/pallas_call | solution.py:175
  310.2 5.3 %collective-permute-start.3 = (bf16[256,512]{1,0:T(8,128)(2,1)}, bf16[256,512]{1,0:T(8,128)(2,1)S(1)}, u32[]{:S(2)}, u32[]{:S(2)}) collective-permute-start(bf16[256,512]{1,0:T(8,128)(2,1)} %get-tuple-element.56), channel_id=1, source_target_pairs={{0,8},{8,16},{16,24},{1,9},{9,17},{17,25},{2,10},{10,18},{18,26},{... | collective-permute-start | bytes 786440 | tf_op jit(solution)/shard_map/ppermute | solution.py:201
  315.5 1.3 collective-permute-done.3
  316.8 0.7 copy-done.7
  317.5 0.0 all-gather.17.cloned.1.call-update
  317.5 2.9 pad_maximum_fusion
  320.5 0.0 copy-done.2
  320.5 3.7 convolution_subtract_fusion.1
  324.2 46.1 %all-gather.17.cloned.1.call-done = bf16[2048,512]{1,0:T(8,128)(2,1)} async-done(((bf16[256,512]{1,0:T(8,128)(2,1)}), bf16[2048,512]{1,0:T(8,128)(2,1)}) %all-gather.17.cloned.1.call-update) | async-done | bytes 2097168 | tf_op jit(solution)/shard_map/all_gather | solution.py:222
  370.3 4.3 %convolution_subtract_fusion = f32[256,2048]{1,0:T(8,128)} fusion(f32[256,2048]{1,0:T(8,128)} %convolution_subtract_fusion.1, bf16[256,512]{1,0:T(8,128)(2,1)S(1)} %copy-done.8, bf16[2048,512]{1,0:T(8,128)(2,1)} %all-gather.17.cloned.1.call-done), kind=kOutput, calls=%fused_computation | convolution fusion | flops 537395200 | bytes 6553600 | tf_op jit(solution)/shard_map/dot_general | solution.py:20
  (13 shorter events, 0.0 us)
Async XLA Ops:
  7.2 4.0 %copy-start.9 = (bf16[256,2048]{1,0:T(8,128)(2,1)S(1)}, bf16[256,2048]{1,0:T(8,128)(2,1)}, u32[]{:S(2)}) copy-start(bf16[256,2048]{1,0:T(8,128)(2,1)} %param.4) | copy-start | bytes 3145732
  7.2 54.8 %all-gather.7.cloned.1.call-start = ((), (), s32[]{:S(2)}) async-start(), calls=%async_computation | async-start | bytes 2359296 | tf_op jit(solution)/shard_map/all_gather | solution.py:208
  9.0 153.0 %all-gather.9.cloned.1.call-start = ((), (), s32[]{:S(2)}) async-start(), calls=%async_computation.1 | async-start | bytes 7077888 | tf_op jit(solution)/shard_map/all_gather | solution.py:209
  11.1 201.9 %all-gather.11.cloned.1.call-start = ((), (), s32[]{:S(2)}) async-start(), calls=%async_computation.2 | async-start | bytes 2359296 | tf_op jit(solution)/shard_map/all_gather | solution.py:222
  103.8 2.6 collective-permute-start
  106.5 0.7 copy-start.5
  107.2 160.5 %all-gather.13.cloned.1.call-start = ((), (), s32[]{:S(2)}) async-start(), calls=%async_computation.3 | async-start | bytes 2359296 | tf_op jit(solution)/shard_map/all_gather | solution.py:222
  167.7 45.3 %copy-start = (f32[256,2048]{1,0:T(8,128)S(1)}, f32[256,2048]{1,0:T(8,128)}, u32[]{:S(2)}) copy-start(f32[256,2048]{1,0:T(8,128)} %param.5) | copy-start | bytes 6291460
  167.7 45.3 %copy-start.6 = (bf16[256,512]{1,0:T(8,128)(2,1)S(1)}, bf16[256,512]{1,0:T(8,128)(2,1)}, u32[]{:S(2)}) copy-start(bf16[256,512]{1,0:T(8,128)(2,1)} %copy-done.5) | copy-start | bytes 786436
  211.7 5.0 %collective-permute-start.1 = (bf16[256,512]{1,0:T(8,128)(2,1)}, bf16[256,512]{1,0:T(8,128)(2,1)S(1)}, u32[]{:S(2)}, u32[]{:S(2)}) collective-permute-start(bf16[256,512]{1,0:T(8,128)(2,1)} %get-tuple-element.36), channel_id=1, source_target_pairs={{0,8},{8,16},{16,24},{1,9},{9,17},{17,25},{2,10},{10,18},{18,26},{... | collective-permute-start | bytes 786440 | tf_op jit(solution)/shard_map/ppermute | solution.py:201
  216.7 0.7 copy-start.3
  217.5 103.0 %all-gather.15.cloned.1.call-start = ((), (), s32[]{:S(2)}) async-start(), calls=%async_computation.4 | async-start | bytes 2359296 | tf_op jit(solution)/shard_map/all_gather | solution.py:222
  217.7 50.0 %copy-start.4 = (bf16[256,512]{1,0:T(8,128)(2,1)S(1)}, bf16[256,512]{1,0:T(8,128)(2,1)}, u32[]{:S(2)}) copy-start(bf16[256,512]{1,0:T(8,128)(2,1)} %copy-done.3) | copy-start | bytes 786436
  260.1 5.4 %collective-permute-start.2 = (bf16[256,512]{1,0:T(8,128)(2,1)}, bf16[256,512]{1,0:T(8,128)(2,1)S(1)}, u32[]{:S(2)}, u32[]{:S(2)}) collective-permute-start(bf16[256,512]{1,0:T(8,128)(2,1)} %get-tuple-element.44), channel_id=1, source_target_pairs={{0,8},{8,16},{16,24},{1,9},{9,17},{17,25},{2,10},{10,18},{18,26},{... | collective-permute-start | bytes 786440 | tf_op jit(solution)/shard_map/ppermute | solution.py:201
  265.4 0.7 copy-start.1
  266.2 104.1 %all-gather.17.cloned.1.call-start = ((), (), s32[]{:S(2)}) async-start(), calls=%async_computation.5 | async-start | bytes 2359296 | tf_op jit(solution)/shard_map/all_gather | solution.py:222
  270.7 46.8 %copy-start.10 = (f32[256,512]{1,0:T(8,128)S(1)}, f32[256,512]{1,0:T(8,128)}, u32[]{:S(2)}) copy-start(f32[256,512]{1,0:T(8,128)} %get-tuple-element.30) | copy-start | bytes 1572868
  310.2 6.6 %collective-permute-start.3 = (bf16[256,512]{1,0:T(8,128)(2,1)}, bf16[256,512]{1,0:T(8,128)(2,1)S(1)}, u32[]{:S(2)}, u32[]{:S(2)}) collective-permute-start(bf16[256,512]{1,0:T(8,128)(2,1)} %get-tuple-element.56), channel_id=1, source_target_pairs={{0,8},{8,16},{16,24},{1,9},{9,17},{17,25},{2,10},{10,18},{18,26},{... | collective-permute-start | bytes 786440 | tf_op jit(solution)/shard_map/ppermute | solution.py:201
  316.8 0.7 copy-start.7
  317.5 2.9 copy-start.2
  320.5 49.8 %copy-start.8 = (bf16[256,512]{1,0:T(8,128)(2,1)S(1)}, bf16[256,512]{1,0:T(8,128)(2,1)}, u32[]{:S(2)}) copy-start(bf16[256,512]{1,0:T(8,128)(2,1)} %copy-done.7) | copy-start | bytes 786436
Sparse Core Ops, SparseCore 0:
  10.1 51.7 all-gather.6
  64.7 97.2 all-gather.8
  164.1 47.3 all-gather.10
  217.6 50.0 all-gather.12
  269.7 49.4 all-gather.14
  321.1 49.0 all-gather.16
